TPU v7x, 32 devices: a whole 2x2x4 slice. The times are simulated.
32 devices in a mesh: region: 16 (over z, y, x), mp: 2 (over core).
Axes of the slice: x: 2, y: 2, z: 4, core: 2. Of those that a mesh axis runs over, the one named last changes fastest.
Arguments:
- grid: bfloat16 [32768, 1024], P('region', 'mp'), may hold values from -6 to 6
- g2m_weight: float32 [32768], P('region'), may hold values from 0.3 to 1
- g2m_slot: int32 [32768], P('region'), may hold values from 0 to 511
- slot_node: int32 [16, 16, 32], P('region'), may hold values from 0 to 511, as said below
- peer_mask: int32 [16, 4], P('region'), may hold values 0 or 1
- norm_gain: float32 [1024], replicated, may hold values from 0.25 to 1.75
- w_qkv: bfloat16 [3, 1024, 1024], P(None, None, 'mp')
- w_out: bfloat16 [1024, 1024], P('mp'), may hold values from -0.1875 to 0.1875
Outputs:
- mesh_state: float32 [8192, 1024], P('region', 'mp')
- grid_out: bfloat16 [32768, 1024], P('region', 'mp')
Inputs may be any that keep to these rules, and one draw needn't show every extreme that they name: `slot_node`: for each mesh tile o and lane c, the entries over all grid tiles r lie in one range b * (16) to (b + 1) * 16 - 1 and name every node of that range, where the range b depends on o and c and different lanes of one mesh tile take different ranges; so every mesh node is named by some send slot, and the 32 slots of one grid tile for one mesh tile name different nodes.
All inputs are finite; a program needn't handle non-finite values. No bound on the sum of `peer_mask` on one device may be relied on, other than what follows from the above.
Results may differ from a plain program's by a relative error of at most 0.006.
Values may be sent and summed in bfloat16 or wider, within the bound.
A program may use at most 192 MiB of HBM per device.

v0:
```python
import functools

import jax
import jax.numpy as jnp
from jax import lax
from jax.experimental import pallas as pl
from jax.experimental.pallas import tpu as pltpu
from jax.sharding import PartitionSpec as P

HEAD_DIM = 64
PAD = 80
PEERS = 4
NEAR, RELAYED = 1, 2
MESH = pl.DeviceIdType.MESH
LOG2E = 1.4426950408889634


def exchange_kernel(n, meanwhile, x_ref, *refs):
    *extra, send, recv, local = refs
    o_ref = extra[-1] if meanwhile is None else extra[-2]
    me = lax.axis_index("region")
    rows = x_ref.shape[0] // n
    barrier = pltpu.get_barrier_semaphore()

    def hello(d, carry):
        pl.semaphore_signal(
            barrier, inc=1, device_id={"region": lax.rem(me + d, n)}, device_id_type=MESH
        )
        return carry

    lax.fori_loop(1, n, hello, 0)
    mine = pl.ds(pl.multiple_of(me * rows, rows), rows)
    own = pltpu.make_async_copy(x_ref.at[mine], o_ref.at[mine], local)
    own.start()
    pl.semaphore_wait(barrier, n - 1)

    def copy(d):
        peer = lax.rem(me + d, n)
        return pltpu.make_async_remote_copy(
            src_ref=x_ref.at[pl.ds(pl.multiple_of(peer * rows, rows), rows)],
            dst_ref=o_ref.at[mine],
            send_sem=send.at[d],
            recv_sem=recv.at[d],
            device_id={"region": peer},
            device_id_type=MESH,
        )

    def begin(d, carry):
        copy(d).start()
        return carry

    def finish(d, carry):
        copy(d).wait()
        return carry

    lax.fori_loop(1, n, begin, 0)
    if meanwhile is not None:
        meanwhile(x_ref, *extra)
    own.wait()
    lax.fori_loop(1, n, finish, 0)


def to_node_order(back_ref, state_ref, hot_ref, _, out_ref):
    low = (state_ref[...] - back_ref[...].astype(jnp.float32)).astype(jnp.bfloat16)
    out_ref[...] = jnp.dot(
        hot_ref[...], back_ref[...], preferred_element_type=jnp.float32
    ) + jnp.dot(hot_ref[...], low, preferred_element_type=jnp.float32)


def exchange(x, n, cid, meanwhile=None, extra_in=(), extra_out=()):
    vmem = pl.BlockSpec(memory_space=pltpu.VMEM)
    return pl.pallas_call(
        functools.partial(exchange_kernel, n, meanwhile),
        out_shape=(jax.ShapeDtypeStruct(x.shape, x.dtype),) + extra_out,
        in_specs=[vmem] * (1 + len(extra_in)),
        out_specs=(vmem,) * (1 + len(extra_out)),
        scratch_shapes=[
            pltpu.SemaphoreType.DMA((n,)),
            pltpu.SemaphoreType.DMA((n,)),
            pltpu.SemaphoreType.DMA,
        ],
        compiler_params=pltpu.CompilerParams(collective_id=cid, has_side_effects=True),
    )(x, *extra_in)


def layer_kernel(
    n, mp, x_ref, gain_ref, w_ref, wo_ref, row_ref, column_ref, state_ref, back_ref,
    gath, nrm, qm, kown, kbuf, vbuf, acc, top, att, out_part, in_part,
    local, psend, precv, msend, mrecv, rsend, rrecv,
):
    region = lax.axis_index("region")
    core = lax.axis_index("mp")
    rows, width = x_ref.shape
    heads = width // HEAD_DIM
    peers = PEERS
    chunk = rows // peers
    blocks = 1 + peers
    barrier = pltpu.get_barrier_semaphore()
    odd = lax.rem(region, 2)
    partner = region + 1 - 2 * odd
    below, above = lax.rem(region - 2 + n, n), lax.rem(region + 2, n)
    far = (peers - 1) * (1 - odd)
    for other in (below, partner, above):
        pl.semaphore_signal(barrier, inc=1, device_id={"region": other}, device_id_type=MESH)
    for j in range(1, mp):
        pl.semaphore_signal(
            barrier, inc=1, device_id={"mp": lax.rem(core + j, mp)}, device_id_type=MESH
        )
    own = pltpu.make_async_copy(x_ref, gath.at[0, core], local)
    own.start()
    acc[...] = jnp.zeros_like(acc)
    top[...] = jnp.full_like(top, -1e30)
    pl.semaphore_wait(barrier, 3 + mp - 1)

    def to_core(s, j):
        return pltpu.make_async_remote_copy(
            src_ref=x_ref if isinstance(s, int) else gath.at[s, core],
            dst_ref=gath.at[s, core],
            send_sem=msend.at[s, j],
            recv_sem=mrecv.at[s, j],
            device_id={"mp": lax.rem(core + j, mp)},
            device_id_type=MESH,
        )

    def to_peer(place, c, other):
        return pltpu.make_async_remote_copy(
            src_ref=x_ref.at[pl.ds(pl.multiple_of(c * chunk, chunk), chunk)],
            dst_ref=gath.at[1 + c, core, pl.ds(place * chunk, chunk)],
            send_sem=psend.at[c, place],
            recv_sem=precv.at[c, place],
            device_id={"region": other},
            device_id_type=MESH,
        )

    direct = ((0, above), (peers - 1, below), (NEAR, partner))

    def to_partner(c):
        return pltpu.make_async_remote_copy(
            src_ref=gath.at[1 + c, core, pl.ds(pl.multiple_of(far * chunk, chunk), chunk)],
            dst_ref=gath.at[1 + c, core, pl.ds(RELAYED * chunk, chunk)],
            send_sem=psend.at[c, RELAYED],
            recv_sem=precv.at[c, RELAYED],
            device_id={"region": partner},
            device_id_type=MESH,
        )

    def arrived(c, place):
        pltpu.make_async_remote_copy(
            src_ref=x_ref.at[pl.ds(0, chunk)],
            dst_ref=gath.at[1 + c, core, pl.ds(pl.multiple_of(place * chunk, chunk), chunk)],
            send_sem=psend.at[c, place],
            recv_sem=precv.at[c, place],
            device_id={"region": partner},
            device_id_type=MESH,
        ).wait_recv()

    for j in range(1, mp):
        to_core(0, j).start()
    for c in range(peers):
        for place, other in direct:
            to_peer(place, c, other).start()
    own.wait()

    def pass_on(s):
        arrived(s - 1, far)
        to_partner(s - 1).start()

    def relay(s):
        arrived(s - 1, peers - 1 - far)
        arrived(s - 1, NEAR)
        arrived(s - 1, RELAYED)
        for j in range(1, mp):
            to_core(s, j).start()

    def block(s, carry):
        for j in range(1, mp):
            to_core(s, j).wait_recv()
        square = jnp.zeros((rows, 1), jnp.float32)
        for m in range(mp):
            part = gath[s, m].astype(jnp.float32)
            square += jnp.sum(part * part, axis=-1, keepdims=True)
        inv = lax.rsqrt(square / (mp * width) + 1e-05)
        for m in range(mp):
            cols = slice(m * width, (m + 1) * width)
            nrm[:, cols] = (gath[s, m].astype(jnp.float32) * inv * gain_ref[:, cols]).astype(
                jnp.bfloat16
            )
        kind = jnp.minimum(s, 1)
        seen = row_ref[kind]

        @pl.when(s == 0)
        def _():
            q = jnp.dot(nrm[...], w_ref[0], preferred_element_type=jnp.float32)
            q = q * (LOG2E * HEAD_DIM ** (-0.5))
            lane = lax.broadcasted_iota(jnp.int32, (rows, 2 * HEAD_DIM), 1)
            for h in range(heads):
                pair = q[:, h // 2 * 2 * HEAD_DIM : (h // 2 + 1) * 2 * HEAD_DIM]
                keep = (lane < HEAD_DIM) if h % 2 == 0 else (lane >= HEAD_DIM)
                qm[h] = jnp.where(keep, pair, 0.0).astype(jnp.bfloat16)

        keys = jnp.dot(nrm[...], w_ref[1], preferred_element_type=jnp.float32)

        @pl.when(s == 0)
        def _():
            kown[...] = keys

        keys = jnp.where(column_ref[kind] > 0, keys, kown[...])
        for g in range(heads // 2):
            kbuf[g] = keys[:, g * 2 * HEAD_DIM : (g + 1) * 2 * HEAD_DIM].astype(jnp.bfloat16)
        vals = jnp.dot(nrm[...], w_ref[2], preferred_element_type=jnp.float32)
        turned = vals.T * seen
        row = lax.broadcasted_iota(jnp.int32, (PAD - HEAD_DIM, rows), 0)
        extra = jnp.where(row == 0, jnp.broadcast_to(seen, row.shape), 0.0).astype(jnp.bfloat16)
        for h in range(heads):
            vbuf[h, :HEAD_DIM] = turned[h * HEAD_DIM : (h + 1) * HEAD_DIM].astype(jnp.bfloat16)
            vbuf[h, HEAD_DIM:] = extra

        @pl.when(jnp.logical_and(s >= 1, s < blocks - 1))
        def _():
            relay(s + 1)

        def two_heads(g, carry):
            key = kbuf[g]
            for e in range(2):
                h = 2 * g + e
                scores = lax.dot_general(
                    key, qm[h], (((1,), (1,)), ((), ())), preferred_element_type=jnp.float32
                )
                old = top[h]
                new = jnp.maximum(old, jnp.max(scores, axis=0, keepdims=True))
                weights = jnp.exp2(scores - new).astype(jnp.bfloat16)
                acc[h] = acc[h] * jnp.exp2(old - new) + jnp.dot(
                    vbuf[h], weights, preferred_element_type=jnp.float32
                )
                top[h] = new
            return carry

        lax.fori_loop(0, heads // 4, two_heads, 0)

        @pl.when(s == 0)
        def _():
            pass_on(s + 1)

        @pl.when(jnp.logical_and(s >= 1, s < blocks - 2))
        def _():
            pass_on(s + 2)

        lax.fori_loop(heads // 4, heads // 2, two_heads, 0)

        @pl.when(s == 0)
        def _():
            relay(s + 1)
            pass_on(s + 2)

        return carry

    lax.fori_loop(0, blocks, block, 0)
    for h in range(heads):
        mix = acc[h]
        att[h * HEAD_DIM : (h + 1) * HEAD_DIM] = mix[:HEAD_DIM] / mix[HEAD_DIM : HEAD_DIM + 1]
    attended = att[...].T.astype(jnp.bfloat16)

    def product(m):
        cols = pl.ds(pl.multiple_of(m * width, width), width)
        return jnp.dot(attended, wo_ref[:, cols], preferred_element_type=jnp.float32)

    def share(j):
        return pltpu.make_async_remote_copy(
            src_ref=out_part.at[j],
            dst_ref=in_part.at[j],
            send_sem=rsend.at[j],
            recv_sem=rrecv.at[j],
            device_id={"mp": lax.rem(core + j, mp)},
            device_id_type=MESH,
        )

    for j in range(1, mp):
        out_part[j] = product(lax.rem(core + j, mp))
        share(j).start()
    total = x_ref[...].astype(jnp.float32) + product(core)
    for j in range(1, mp):
        share(j).wait()
        total += in_part[j]
    state_ref[...] = total
    back_ref[...] = total.astype(jnp.bfloat16)
    for c in range(peers):
        for place, other in direct:
            to_peer(place, c, other).wait_send()
        to_partner(c).wait_send()

    def drain(s, carry):
        for j in range(1, mp):
            to_core(s, j).wait_send()
        return carry

    lax.fori_loop(0, blocks, drain, 0)


def layer(x, gain, w_qkv, w_out, row_mask, column_mask, n, mp, cid):
    rows, width = x.shape
    heads = width // HEAD_DIM
    peers = PEERS
    blocks = 1 + peers
    bf16, f32 = jnp.bfloat16, jnp.float32
    vmem = pl.BlockSpec(memory_space=pltpu.VMEM)
    dma = pltpu.SemaphoreType.DMA
    return pl.pallas_call(
        functools.partial(layer_kernel, n, mp),
        out_shape=(
            jax.ShapeDtypeStruct((rows, width), f32),
            jax.ShapeDtypeStruct((rows, width), bf16),
        ),
        in_specs=[vmem] * 6,
        out_specs=(vmem, vmem),
        scratch_shapes=[
            pltpu.VMEM((blocks, mp, rows, width), bf16),
            pltpu.VMEM((rows, mp * width), bf16),
            pltpu.VMEM((heads, rows, 2 * HEAD_DIM), bf16),
            pltpu.VMEM((rows, width), f32),
            pltpu.VMEM((heads // 2, rows, 2 * HEAD_DIM), bf16),
            pltpu.VMEM((heads, PAD, rows), bf16),
            pltpu.VMEM((heads, PAD, rows), f32),
            pltpu.VMEM((heads, 1, rows), f32),
            pltpu.VMEM((width, rows), f32),
            pltpu.VMEM((mp, rows, width), f32),
            pltpu.VMEM((mp, rows, width), f32),
            dma,
            dma((peers, peers)),
            dma((peers, peers)),
            dma((blocks, mp)),
            dma((blocks, mp)),
            dma((mp,)),
            dma((mp,)),
        ],
        compiler_params=pltpu.CompilerParams(
            collective_id=cid, has_side_effects=True, vmem_limit_bytes=56 * 1024 * 1024
        ),
    )(x, gain, w_qkv, w_out, row_mask, column_mask)


def on_device(n, mp, grid, g2m_weight, g2m_slot, slot_node, peer_mask, norm_gain, w_qkv, w_out):
    cap = slot_node.shape[2]
    slots = n * cap
    scaled = (g2m_weight[:, None] * grid.astype(jnp.float32)).astype(jnp.bfloat16)
    slot_hot = (g2m_slot[None, :] == jnp.arange(slots, dtype=jnp.int32)[:, None]).astype(
        jnp.bfloat16
    )
    partial_value = jnp.dot(slot_hot, scaled, preferred_element_type=jnp.float32).astype(
        jnp.bfloat16
    )
    (mesh_in,) = exchange(partial_value, n, 0)
    two_below, below, above, two_above = (peer_mask[0, c : c + 1] for c in range(PEERS))
    odd = lax.axis_index("region") % 2 == 1
    places = jnp.concatenate(
        [two_below, jnp.where(odd, below, above), jnp.where(odd, above, below), two_above]
    )
    peer_seen = jnp.repeat(places.astype(jnp.float32), slots // PEERS)
    seen = jnp.stack([jnp.ones_like(peer_seen), peer_seen])
    state, back = layer(
        mesh_in, norm_gain[None, :], w_qkv, w_out, seen[:, None, :], seen[:, :, None], n, mp, 1
    )
    flat_nodes = slot_node[0].reshape(-1)
    node_hot = (jnp.arange(slots, dtype=jnp.int32)[:, None] == flat_nodes[None, :]).astype(
        jnp.bfloat16
    )
    returned, mesh_state = exchange(
        back,
        n,
        2,
        to_node_order,
        (state, node_hot),
        (jax.ShapeDtypeStruct(state.shape, state.dtype),),
    )
    gathered = jnp.dot(slot_hot.T, returned, preferred_element_type=jnp.float32)
    grid_out = (grid.astype(jnp.float32) + gathered).astype(jnp.bfloat16)
    return (mesh_state, grid_out)


def solution(mesh):
    return jax.shard_map(
        functools.partial(on_device, mesh.shape["region"], mesh.shape["mp"]),
        mesh=mesh,
        in_specs=(
            P("region", "mp"),
            P("region"),
            P("region"),
            P("region", None, None),
            P("region", None),
            P(),
            P(None, None, "mp"),
            P("mp", None),
        ),
        out_specs=(P("region", "mp"), P("region", "mp")),
        check_vma=False,
    )
```

profile of v0, /device:TPU:12, one launch (start us, length us, event | category | flops | bytes accessed | tf_op | source)
XLA Modules:
  0.0 113.9 jit_solution(12410589085702222571)
XLA Ops:
  0.6 0.8 eq.38
  1.4 1.5 %fusion.12 = (s32[1,1]{1,0:T(1,128)}, s32[1,1]{1,0:T(1,128)}, s32[1,1]{1,0:T(1,128)}, s32[1,1]{1,0:T(1,128)}) fusion(s32[1,4]{1,0:T(1,128)} %param.12), kind=kLoop, calls=%fused_computation.15 | loop fusion | bytes 32 | tf_op jit(solution)/shard_map/slice | solution.py:352
  5.3 1.4 %add_convert_fusion = f32[4]{0:T(128)S(1)} fusion(s32[1]{0:T(128)} %bitcast.5, s32[1]{0:T(128)S(6)} %select_n.22, s32[1]{0:T(128)S(6)} %select_n.21, s32[1]{0:T(128)} %bitcast.1), kind=kLoop, calls=%fused_computation.13 | loop fusion | flops 16 | bytes 32 | tf_op jit(solution)/shard_map/convert_element_type | solution.py:357
  6.7 0.1 broadcast_in_dim.17
  6.8 0.6 broadcast_in_dim.18.row_ref
  7.4 1.0 copy.11.column_ref
  8.4 0.9 fusion.11.refs_1_
  9.4 3.7 %fusion.8.x_ref = bf16[512,512]{1,0:T(8,128)(2,1)} fusion(bf16[2048,512]{1,0:T(8,128)(2,1)} %param.8, f32[2048]{0:T(1024)} %param.9, s32[2048]{0:T(1024)} %param.10), kind=kOutput, calls=%fused_computation.10 | convolution fusion | flops 1078198272 | bytes 2637824 | tf_op jit(solution)/shard_map/dot_general | solution.py:348
  13.1 18.7 %shard_map.95.x_ref = bf16[512,512]{1,0:T(8,128)(2,1)} custom-call(bf16[512,512]{1,0:T(8,128)(2,1)} %fusion.8.x_ref), custom_call_target="tpu_custom_call" | custom-call | tf_op jit(solution)/shard_map/pallas_call | solution.py:72
  31.8 0.0 copy-start.1
  31.8 0.0 copy-start.2
  31.8 58.0 %shard_map.96 = (f32[512,512]{1,0:T(8,128)}, bf16[512,512]{1,0:T(8,128)(2,1)}) custom-call(bf16[512,512]{1,0:T(8,128)(2,1)} %shard_map.95.x_ref, f32[1,1024]{1,0:T(1,128)} %bitcast.11, bf16[3,1024,512]{2,1,0:T(8,128)(2,1)} %w_ref.1, bf16[512,1024]{1,0:T(8,128)(2,1)} %wo_ref.1, f32[2,1,512]{2,1,0:T(1,128)} %broadcast_in_dim.18.row_ref, ...), custom_call_target="tpu_custom_call" | custom-call | tf_op jit(solution)/shard_map/pallas_call | solution.py:307
  89.9 19.1 %shard_map.97 = (bf16[512,512]{1,0:T(8,128)(2,1)}, f32[512,512]{1,0:T(8,128)}) custom-call(bf16[512,512]{1,0:T(8,128)(2,1)} %get-tuple-element.6.x_ref, f32[512,512]{1,0:T(8,128)} %get-tuple-element.7.refs_0_, bf16[512,512]{1,0:T(8,128)(2,1)} %fusion.11.refs_1_), custom_call_target="tpu_custom_call" | custom-call | tf_op jit(solution)/shard_map/pallas_call | solution.py:72
  108.9 0.0 copy-done.1
  109.0 0.0 copy-done.2
  109.0 0.0 copy-start
  109.0 3.9 %fusion.1 = bf16[2048,512]{1,0:T(8,128)(2,1)} fusion(bf16[2048,512]{1,0:T(8,128)(2,1)S(1)} %copy-done.1, bf16[512,512]{1,0:T(8,128)(2,1)} %get-tuple-element.9, s32[2048]{0:T(1024)S(1)} %copy-done.2), kind=kOutput, calls=%fused_computation.3 | convolution fusion | flops 1077936128 | bytes 4726784 | tf_op jit(solution)/shard_map/dot_general | solution.py:374
  112.9 0.0 copy-done
  112.9 1.0 copy.13
  (1 shorter events, 0.0 us)
Async XLA Ops:
  31.8 77.1 %copy-start.1 = (bf16[2048,512]{1,0:T(8,128)(2,1)S(1)}, bf16[2048,512]{1,0:T(8,128)(2,1)}, u32[]{:S(2)}) copy-start(bf16[2048,512]{1,0:T(8,128)(2,1)} %param.8) | copy-start | bytes 6291460
  31.8 77.1 %copy-start.2 = (s32[2048]{0:T(1024)S(1)}, s32[2048]{0:T(1024)}, u32[]{:S(2)}) copy-start(s32[2048]{0:T(1024)} %param.10) | copy-start | bytes 24580
  109.0 3.9 %copy-start = (f32[512,512]{1,0:T(8,128)S(1)}, f32[512,512]{1,0:T(8,128)}, u32[]{:S(2)}) copy-start(f32[512,512]{1,0:T(8,128)} %get-tuple-element.18) | copy-start | bytes 3145732
where the time goes:
time: 114 us
  Pallas kernels  95.8 us (84%)
  matrix products  7.64 us (7%)
  local copies, waits for them, and re-layouts  4.94 us (4%)
  between operations  3.13 us (3%)
  other arithmetic  2.35 us (2%)
    pallas_call x1, Pallas kernels, layer(): pl.pallas_call(functools.partial(layer_kernel, n, mp), out_shape=(jax.Sha...  58 us
    pallas_call x2, Pallas kernels, exchange(): pl.pallas_call(functools.partial(exchange_kernel, n, meanwhile), out_shap...  37.8 us
    dot_general x1, matrix products, on_device(): gathered = jnp.dot(slot_hot.T, returned, preferred_element_type=jnp.float32)  3.91 us
    dot_general x1, matrix products, on_device(): jnp.dot(slot_hot, scaled, preferred_element_type=jnp.float32)  3.73 us

commit v1 on v0

v1 whole, which is shorter than its diff:
```python
import functools

import jax
import jax.numpy as jnp
from jax import lax
from jax.experimental import pallas as pl
from jax.experimental.pallas import tpu as pltpu
from jax.sharding import PartitionSpec as P

HEAD_DIM = 64
PAD = 80
PEERS = 4
Y, NEAR, RELAYED, Z = range(PEERS)
MESH = pl.DeviceIdType.MESH
LOG2E = 1.4426950408889634
NT = (((1,), (1,)), ((), ()))


def window_kernel(
    n, mp, grid_ref, weight_ref, slot_ref, node_ref, peer_ref, gain_ref, w_ref, wo_ref,
    mesh_ref, returned_ref,
    points, wcol, scaled, part, xg, gath, wbuf, wobuf, wvt, hot, rowm, colm,
    qm, kown, kbuf, vbuf, sbuf, acc, top, attb, out_part, in_part, total, state, back, ordered,
    local, gsem, wsem, asend, arecv, xsend, xrecv, psend, precv, msend, mrecv, rsend, rrecv,
    bsend, brecv,
):
    f32, bf16 = jnp.float32, jnp.bfloat16
    region = lax.axis_index("region")
    core = lax.axis_index("mp")
    count, width = points.shape
    rows = xg.shape[1]
    cap = rows // n
    heads = width // HEAD_DIM
    peers = PEERS
    chunk = rows // peers
    blocks = 1 + peers
    half = rows // 2
    piece = count // peers
    odd = lax.rem(region, 2)
    far = lax.rem(region // 2, 2)
    step = 2 - 4 * odd
    partner = region + 1 - 2 * odd
    across = region + 2 - 4 * far
    beyond = lax.rem(region + 4 - 8 * far + n, n)
    second = lax.rem(region + step + n, n)
    relay_place = jnp.where(odd == far, Y, Z)
    cols = pl.ds(pl.multiple_of(core * width, width), width)

    loads = [
        pltpu.make_async_copy(
            grid_ref.at[pl.ds(k * piece, piece)], points.at[pl.ds(k * piece, piece)], gsem.at[k]
        )
        for k in range(peers)
    ]
    for load in loads:
        load.start()
    weights = [
        pltpu.make_async_copy(w_ref, wbuf, wsem.at[0]),
        pltpu.make_async_copy(wo_ref, wobuf, wsem.at[1]),
    ]
    for load in weights:
        load.start()

    barrier = pltpu.get_barrier_semaphore()

    def hello(d, carry):
        pl.semaphore_signal(
            barrier, inc=1, device_id={"region": lax.rem(region + d, n)}, device_id_type=MESH
        )
        return carry

    lax.fori_loop(1, n, hello, 0)
    for j in range(1, mp):
        pl.semaphore_signal(
            barrier, inc=1, device_id={"mp": lax.rem(core + j, mp)}, device_id_type=MESH
        )

    wcol[...] = jnp.broadcast_to(weight_ref[...], (8, count)).T
    for k in range(peers):
        loads[k].wait()
        span = slice(k * piece, (k + 1) * piece)
        scaled[span] = (wcol[span, 0:1] * points[span].astype(f32)).astype(bf16)

    def mine_of(ref):
        return ref.at[pl.ds(pl.multiple_of(region * cap, cap), cap)]

    def base_of(j):
        return region + n // 4 + j * (n // 2)

    def scatter(j):
        place = lax.broadcasted_iota(jnp.int32, (half, 1), 0)
        ids = lax.rem(place // cap + base_of(j), n) * cap + lax.rem(place, cap)
        part[j] = jnp.dot(
            jnp.where(ids == slot_ref[...], 1.0, 0.0).astype(bf16),
            scaled[...],
            preferred_element_type=f32,
        ).astype(bf16)

    def sow(j, k):
        return pltpu.make_async_remote_copy(
            src_ref=part.at[j, pl.ds(pl.multiple_of(k * cap, cap), cap)],
            dst_ref=mine_of(xg.at[core]),
            send_sem=asend.at[j * (n // 2) + k],
            recv_sem=arecv.at[region],
            device_id={"region": lax.rem(base_of(j) + k, n)},
            device_id_type=MESH,
        )

    def sow_all(j, lo, hi):
        def go(k, carry):
            sow(j, k).start()
            return carry

        lax.fori_loop(lo, hi, go, 0)

    scatter(0)
    pl.semaphore_wait(barrier, n - 1 + mp - 1)
    sow_all(0, 0, n // 2)
    scatter(1)
    sow_all(1, 0, n // 4)
    sow_all(1, n // 4 + 1, n // 2)
    own = pltpu.make_async_copy(
        part.at[1, pl.ds(n // 4 * cap, cap)], mine_of(xg.at[core]), local.at[0]
    )
    own.start()

    acc[...] = jnp.zeros_like(acc)
    top[...] = jnp.full_like(top, -1e30)
    seen = [peer_ref[0, i].astype(f32) for i in range(4)]
    shown = {
        Y: jnp.where(far == 0, seen[3], seen[0]),
        Z: jnp.where(far == 0, seen[0], seen[3]),
        NEAR: jnp.where(odd == 0, seen[2], seen[1]),
        RELAYED: jnp.where(odd == 0, seen[1], seen[2]),
    }
    for ref, axis in ((rowm, 1), (colm, 0)):
        shape = ref.shape[1:]
        place = lax.broadcasted_iota(jnp.int32, shape, axis) // chunk
        mask = jnp.zeros(shape, f32)
        for p in range(peers):
            mask = jnp.where(place == p, shown[p], mask)
        ref[0] = jnp.ones(shape, f32)
        ref[1] = mask
    lane = lax.broadcasted_iota(jnp.int32, (n, rows), 1)
    spread = jnp.zeros((n, rows), jnp.int32)
    for c in range(cap):
        spread = jnp.where(lax.rem(lane, cap) == c, node_ref[0, :, c : c + 1], spread)
    owner = lax.broadcasted_iota(jnp.int32, (n, rows), 0)
    flat = jnp.sum(jnp.where(lane // cap == owner, spread, 0), axis=0, keepdims=True)
    hot[...] = jnp.where(
        lax.broadcasted_iota(jnp.int32, (rows, rows), 0) == flat, 1.0, 0.0
    ).astype(bf16)
    for load in weights:
        load.wait()
    wvt[...] = wbuf[2].T
    own.wait()

    def x_to_core(q, j):
        span = pl.ds(pl.multiple_of(q * chunk, chunk), chunk)
        return pltpu.make_async_remote_copy(
            src_ref=xg.at[core, span],
            dst_ref=xg.at[core, span],
            send_sem=xsend.at[q, j],
            recv_sem=xrecv.at[q, j],
            device_id={"mp": lax.rem(core + j, mp)},
            device_id_type=MESH,
        )

    def reaped(q, carry):
        def one(k, c):
            source = q * (n // peers) + k

            @pl.when(source != region)
            def _():
                pltpu.make_async_remote_copy(
                    src_ref=part.at[0, pl.ds(0, cap)],
                    dst_ref=xg.at[core, pl.ds(pl.multiple_of(source * cap, cap), cap)],
                    send_sem=asend.at[0],
                    recv_sem=arecv.at[source],
                    device_id={"region": partner},
                    device_id_type=MESH,
                ).wait_recv()

            return c

        lax.fori_loop(0, n // peers, one, 0)
        for j in range(1, mp):
            x_to_core(q, j).start()
        return carry

    lax.fori_loop(0, peers, reaped, 0)

    def send(c, place, source, other):
        return pltpu.make_async_remote_copy(
            src_ref=source,
            dst_ref=gath.at[1 + c, pl.ds(place * chunk, chunk), cols],
            send_sem=psend.at[c, place],
            recv_sem=precv.at[c, place],
            device_id={"region": other},
            device_id_type=MESH,
        )

    def own_chunk(c):
        return gath.at[0, pl.ds(pl.multiple_of(c * chunk, chunk), chunk), cols]

    def held(c, place):
        return gath.at[1 + c, pl.ds(pl.multiple_of(place * chunk, chunk), chunk), cols]

    def to_near(c):
        return send(c, NEAR, own_chunk(c), partner)

    def to_across(c):
        return send(c, Y, own_chunk(c), across)

    def forward(c):
        return send(c, Z, held(c, Y), beyond)

    def relay(c):
        if c % 2 == 0:
            return send(c, RELAYED, held(c, NEAR), second)
        return send(c, RELAYED, held(c, relay_place), partner)

    def arrived(c, place):
        pltpu.make_async_remote_copy(
            src_ref=own_chunk(0),
            dst_ref=held(c, place),
            send_sem=psend.at[c, place],
            recv_sem=precv.at[c, place],
            device_id={"region": partner},
            device_id_type=MESH,
        ).wait_recv()

    def normalise(q, carry):
        for j in range(1, mp):
            x_to_core(q, j).wait_recv()
        span = pl.ds(pl.multiple_of(q * chunk, chunk), chunk)
        square = jnp.zeros((chunk, 1), f32)
        for m in range(mp):
            value = xg[m, span].astype(f32)
            square += jnp.sum(value * value, axis=-1, keepdims=True)
        inv = lax.rsqrt(square / (mp * width) + 1e-05)
        for m in range(mp):
            at = slice(m * width, (m + 1) * width)
            gath[0, span, at] = (xg[m, span].astype(f32) * inv * gain_ref[:, at]).astype(bf16)
        to_across(q).start()
        to_near(q).start()
        return carry

    lax.fori_loop(0, peers, normalise, 0)

    def to_core(s, j):
        return pltpu.make_async_remote_copy(
            src_ref=gath.at[s, :, cols],
            dst_ref=gath.at[s, :, cols],
            send_sem=msend.at[s, j],
            recv_sem=mrecv.at[s, j],
            device_id={"mp": lax.rem(core + j, mp)},
            device_id_type=MESH,
        )

    def complete(s):
        for j in range(1, mp):
            to_core(s, j).start()

    def block(s, carry):
        @pl.when(s > 0)
        def _():
            for j in range(1, mp):
                to_core(s, j).wait_recv()

        kind = jnp.minimum(s, 1)
        seen = rowm[kind]
        keys = jnp.dot(gath[s], wbuf[1], preferred_element_type=f32)

        @pl.when(s == 0)
        def _():
            kown[...] = keys
            q = jnp.dot(gath[0], wbuf[0], preferred_element_type=f32)
            q = q * (LOG2E * HEAD_DIM ** (-0.5))
            lane = lax.broadcasted_iota(jnp.int32, (rows, 2 * HEAD_DIM), 1)
            for h in range(heads):
                pair = q[:, h // 2 * 2 * HEAD_DIM : (h // 2 + 1) * 2 * HEAD_DIM]
                keep = (lane < HEAD_DIM) if h % 2 == 0 else (lane >= HEAD_DIM)
                qm[h] = jnp.where(keep, pair, 0.0).astype(bf16)

        kbuf[...] = jnp.where(colm[kind] > 0, keys, kown[...]).astype(bf16)
        turned = lax.dot_general(wvt[...], gath[s], NT, preferred_element_type=f32) * seen
        row = lax.broadcasted_iota(jnp.int32, (PAD - HEAD_DIM, rows), 0)
        extra = jnp.where(row == 0, jnp.broadcast_to(seen, row.shape), 0.0).astype(bf16)
        for h in range(heads):
            vbuf[h, :HEAD_DIM] = turned[h * HEAD_DIM : (h + 1) * HEAD_DIM].astype(bf16)
            vbuf[h, HEAD_DIM:] = extra

        def scores(h, c):
            span = slice(c * half, (c + 1) * half)
            value = lax.dot_general(
                kbuf[span, h // 2 * 2 * HEAD_DIM : (h // 2 + 1) * 2 * HEAD_DIM],
                qm[h],
                NT,
                preferred_element_type=f32,
            )
            sbuf[h % 2, span] = value
            return jnp.max(value.reshape(half // 8, 8, rows), axis=0)

        peak = jnp.maximum(scores(0, 0), scores(0, 1))
        for h in range(heads):
            old = top[h]
            new = jnp.maximum(old, jnp.max(peak, axis=0, keepdims=True))
            top[h] = new
            summed, after = None, None
            for c in range(2):
                if h + 1 < heads:
                    value = scores(h + 1, c)
                    after = value if after is None else jnp.maximum(after, value)
                span = slice(c * half, (c + 1) * half)
                ahead = jnp.exp2(sbuf[h % 2, span] - new).astype(bf16)
                value = jnp.dot(vbuf[h, :, span], ahead, preferred_element_type=f32)
                summed = value if summed is None else summed + value
            acc[h] = acc[h] * jnp.exp2(old - new) + summed
            peak = after
            if h == heads // 2 - 1:
                for c in range(1, peers):

                    @pl.when(s == c)
                    def _(c=c):
                        if c == 1:
                            arrived(c, NEAR)
                        if c == 3:
                            arrived(c, NEAR)
                        arrived_rest(c)
                        complete(c + 1)

        @pl.when(s == 0)
        def _():
            arrived(0, Y)
            forward(0).start()
            arrived(0, NEAR)
            relay(0).start()
            arrived(1, Y)
            forward(1).start()
            arrived(2, Y)
            forward(2).start()
            arrived(2, NEAR)
            relay(2).start()
            early(1)
            arrived(0, Z)
            arrived(0, RELAYED)
            complete(1)
            arrived(3, Y)
            forward(3).start()

        @pl.when(s == 1)
        def _():
            early(3)

        return carry

    def early(c):
        @pl.when(relay_place == Z)
        def _():
            arrived(c, Z)

        relay(c).start()

    def arrived_rest(c):
        if c % 2 == 0:
            arrived(c, Z)
        else:

            @pl.when(relay_place != Z)
            def _():
                arrived(c, Z)

        arrived(c, RELAYED)

    lax.fori_loop(0, blocks, block, 0)
    for h in range(heads):
        mix = acc[h]
        attb[h * HEAD_DIM : (h + 1) * HEAD_DIM] = mix[:HEAD_DIM] / mix[HEAD_DIM : HEAD_DIM + 1]
    total[...] = attb[...].T.astype(bf16)

    first = 1 - region * 2 // n

    def half_of(h):
        return first if h == 0 else 1 - first

    def span_of(h):
        return pl.ds(pl.multiple_of(half_of(h) * half, half), half)

    def product(h, m):
        at = pl.ds(pl.multiple_of(m * width, width), width)
        return jnp.dot(total[span_of(h)], wobuf[:, at], preferred_element_type=f32)

    def share(h, j):
        return pltpu.make_async_remote_copy(
            src_ref=out_part.at[h, j],
            dst_ref=in_part.at[h, j],
            send_sem=rsend.at[h, j],
            recv_sem=rrecv.at[h, j],
            device_id={"mp": lax.rem(core + j, mp)},
            device_id_type=MESH,
        )

    def give(k):
        return pltpu.make_async_remote_copy(
            src_ref=back.at[pl.ds(pl.multiple_of(k * cap, cap), cap)],
            dst_ref=mine_of(returned_ref),
            send_sem=bsend.at[k],
            recv_sem=brecv.at[region],
            device_id={"region": k},
            device_id_type=MESH,
        )

    for h in range(2):
        for j in range(1, mp):
            out_part[h, j] = product(h, lax.rem(core + j, mp))
            share(h, j).start()
        span = span_of(h)
        state[span] = xg[core, span].astype(f32) + product(h, core)
    for h in range(2):
        span = span_of(h)
        value = state[span]
        for j in range(1, mp):
            share(h, j).wait_recv()
            value += in_part[h, j]
        state[span] = value
        back[span] = value.astype(bf16)

        def go(k, carry, h=h):
            other = half_of(h) * (n // 2) + k

            @pl.when(other != region)
            def _():
                give(other).start()

            return carry

        lax.fori_loop(0, n // 2, go, 0)

    keep = pltpu.make_async_copy(mine_of(back), mine_of(returned_ref), local.at[1])
    keep.start()
    low = (state[...] - back[...].astype(f32)).astype(bf16)
    ordered[...] = jnp.dot(hot[...], back[...], preferred_element_type=f32) + jnp.dot(
        hot[...], low, preferred_element_type=f32
    )
    out = pltpu.make_async_copy(ordered, mesh_ref, local.at[2])
    out.start()

    def drain(k, carry):
        for j in range(2):

            @pl.when(j * (n // 2) + k != n // 2 + n // 4)
            def _(j=j):
                sow(j, k).wait_send()

        return carry

    lax.fori_loop(0, n // 2, drain, 0)
    for c in range(peers):
        for j in range(1, mp):
            x_to_core(c, j).wait_send()
            to_core(c + 1, j).wait_send()
        for copy in (to_near, to_across, forward, relay):
            copy(c).wait_send()
    for h in range(2):
        for j in range(1, mp):
            share(h, j).wait_send()
    keep.wait()

    def finish(k, carry):
        @pl.when(k != region)
        def _():
            give(k).wait_send()
            pltpu.make_async_remote_copy(
                src_ref=back.at[pl.ds(0, cap)],
                dst_ref=returned_ref.at[pl.ds(pl.multiple_of(k * cap, cap), cap)],
                send_sem=bsend.at[k],
                recv_sem=brecv.at[k],
                device_id={"region": partner},
                device_id_type=MESH,
            ).wait_recv()

        return carry

    lax.fori_loop(0, n, finish, 0)
    out.wait()


def window(grid, weight, slot, nodes, peer_mask, gain, w_qkv, w_out, n, mp, cid):
    count, width = grid.shape
    rows = nodes.shape[1] * nodes.shape[2]
    depth = w_qkv.shape[1]
    heads = width // HEAD_DIM
    peers = PEERS
    chunk = rows // peers
    blocks = 1 + peers
    half = rows // 2
    bf16, f32 = jnp.bfloat16, jnp.float32
    vmem = pl.BlockSpec(memory_space=pltpu.VMEM)
    far = pl.BlockSpec(memory_space=pl.ANY)
    scalar = pl.BlockSpec(memory_space=pltpu.SMEM)
    dma = pltpu.SemaphoreType.DMA
    return pl.pallas_call(
        functools.partial(window_kernel, n, mp),
        out_shape=(
            jax.ShapeDtypeStruct((rows, width), f32),
            jax.ShapeDtypeStruct((rows, width), bf16),
        ),
        in_specs=[far, vmem, vmem, vmem, scalar, vmem, far, far],
        out_specs=(far, vmem),
        scratch_shapes=[
            pltpu.VMEM((count, width), bf16),
            pltpu.VMEM((count, 8), f32),
            pltpu.VMEM((count, width), bf16),
            pltpu.VMEM((2, half, width), bf16),
            pltpu.VMEM((mp, rows, width), bf16),
            pltpu.VMEM((blocks, rows, mp * width), bf16),
            pltpu.VMEM((3, depth, width), bf16),
            pltpu.VMEM((width, depth), bf16),
            pltpu.VMEM((width, depth), bf16),
            pltpu.VMEM((rows, rows), bf16),
            pltpu.VMEM((2, 1, rows), f32),
            pltpu.VMEM((2, rows, 1), f32),
            pltpu.VMEM((heads, rows, 2 * HEAD_DIM), bf16),
            pltpu.VMEM((rows, width), f32),
            pltpu.VMEM((rows, width), bf16),
            pltpu.VMEM((heads, PAD, rows), bf16),
            pltpu.VMEM((2, rows, rows), f32),
            pltpu.VMEM((heads, PAD, rows), f32),
            pltpu.VMEM((heads, 1, rows), f32),
            pltpu.VMEM((width, rows), f32),
            pltpu.VMEM((2, mp, half, width), f32),
            pltpu.VMEM((2, mp, half, width), f32),
            pltpu.VMEM((rows, width), bf16),
            pltpu.VMEM((rows, width), f32),
            pltpu.VMEM((rows, width), bf16),
            pltpu.VMEM((rows, width), f32),
            dma((3,)),
            dma((peers,)),
            dma((2,)),
            dma((n,)),
            dma((n,)),
            dma((peers, mp)),
            dma((peers, mp)),
            dma((peers, peers)),
            dma((peers, peers)),
            dma((blocks, mp)),
            dma((blocks, mp)),
            dma((2, mp)),
            dma((2, mp)),
            dma((n,)),
            dma((n,)),
        ],
        compiler_params=pltpu.CompilerParams(
            collective_id=cid, has_side_effects=True, vmem_limit_bytes=60 * 1024 * 1024
        ),
    )(grid, weight, slot, nodes, peer_mask, gain, w_qkv, w_out)


def on_device(n, mp, grid, g2m_weight, g2m_slot, slot_node, peer_mask, norm_gain, w_qkv, w_out):
    mesh_state, returned = window(
        grid, g2m_weight[None, :], g2m_slot[None, :], slot_node, peer_mask, norm_gain[None, :],
        w_qkv, w_out, n, mp, 0,
    )
    slots = returned.shape[0]
    slot_hot = (g2m_slot[None, :] == jnp.arange(slots, dtype=jnp.int32)[:, None]).astype(
        jnp.bfloat16
    )
    gathered = jnp.dot(slot_hot.T, returned, preferred_element_type=jnp.float32)
    grid_out = (grid.astype(jnp.float32) + gathered).astype(jnp.bfloat16)
    return (mesh_state, grid_out)


def solution(mesh):
    return jax.shard_map(
        functools.partial(on_device, mesh.shape["region"], mesh.shape["mp"]),
        mesh=mesh,
        in_specs=(
            P("region", "mp"),
            P("region"),
            P("region"),
            P("region", None, None),
            P("region", None),
            P(),
            P(None, None, "mp"),
            P("mp", None),
        ),
        out_specs=(P("region", "mp"), P("region", "mp")),
        check_vma=False,
    )
```

time: 114 us -> 79.6 us (0.70)
  Pallas kernels: 95.8 us -> 73.6 us
  local copies, waits for them, and re-layouts: 4.94 us -> 0.98 us
  matrix products: 7.64 us -> 3.92 us
  between operations: 3.13 us -> 0.68 us
  other arithmetic: 2.35 us -> 0 us
    pallas_call x3 -> x1, Pallas kernels: 95.8 us -> 73.6 us  [window(): pl.pallas_call(functools.partial(window_kernel, n, mp), out_shape=(jax.Sh...]
    dot_general x1 -> x0, matrix products: 3.73 us -> none  [on_device(): jnp.dot(slot_hot, scaled, preferred_element_type=jnp.float32)]
    convert_element_type x2 -> x0, other arithmetic: 2.35 us -> none  [the longest x1 1.41 us: on_device(): peer_seen = jnp.repeat(places.astype(jnp.float32), slots // PEERS)]
    broadcast_in_dim x4 -> x0, local copies, waits for them, and re-layouts: 1.71 us -> none  [the longest x2 1.04 us: on_device(): seen[:, :, None]]
    slice x1 -> x0, local copies, waits for them, and re-layouts: 1.47 us -> none  [on_device(): peer_mask[0, c:c + 1]]
where the time goes in v1:
time: 79.6 us; the launch traced here: 79.2 us
  Pallas kernels  73.6 us (92%)
  matrix products  3.92 us (5%)
  local copies, waits for them, and re-layouts  0.98 us (1%)
    pallas_call x1, Pallas kernels, window(): pl.pallas_call(functools.partial(window_kernel, n, mp), out_shape=(jax.Sh...  73.6 us
    dot_general x1, matrix products, on_device(): gathered = jnp.dot(slot_hot.T, returned, preferred_element_type=jnp.float32)  3.92 us

profile of v1, /device:TPU:12, one launch (start us, length us, event | category | flops | bytes accessed | tf_op | source)
XLA Modules:
  0.0 79.2 jit_solution(10253969204430270198)
XLA Ops:
  0.6 0.0 copy-start
  0.6 0.0 copy-start.2
  0.7 73.6 %shard_map.95 = (f32[512,512]{1,0:T(8,128)}, bf16[512,512]{1,0:T(8,128)(2,1)}) custom-call(bf16[2048,512]{1,0:T(8,128)(2,1)} %grid_ref.1, f32[1,2048]{1,0:T(1,128)} %bitcast.4, s32[1,2048]{1,0:T(1,128)} %bitcast.5, s32[1,16,32]{2,1,0:T(8,128)} %node_ref.1, s32[1,4]{1,0:T(1,128)} %peer_ref.1, f32[1,1024]{1,0:T(1,128)} %bitcast.6, ...), custom_call_target="tpu_custom_call" | custom-call | tf_op jit(solution)/shard_map/pallas_call | solution.py:503
  74.2 0.0 copy-done
  74.3 0.0 copy-done.2
  74.3 0.0 copy-start.1
  74.3 3.9 %add_convert_fusion = bf16[2048,512]{1,0:T(8,128)(2,1)} fusion(bf16[2048,512]{1,0:T(8,128)(2,1)S(1)} %copy-done, bf16[512,512]{1,0:T(8,128)(2,1)} %get-tuple-element.5, s32[2048]{0:T(1024)S(1)} %copy-done.2), kind=kOutput, calls=%fused_computation | convolution fusion | flops 1077936128 | bytes 4726784 | tf_op jit(solution)/shard_map/dot_general | solution.py:569
  78.2 0.0 copy-done.1
  78.2 1.0 %copy.11 = f32[512,512]{1,0:T(8,128)} copy(f32[512,512]{1,0:T(8,128)S(1)} %copy-done.1) | data formatting | bytes 2097152
Async XLA Ops:
  0.6 73.6 %copy-start = (bf16[2048,512]{1,0:T(8,128)(2,1)S(1)}, bf16[2048,512]{1,0:T(8,128)(2,1)}, u32[]{:S(2)}) copy-start(bf16[2048,512]{1,0:T(8,128)(2,1)} %grid_ref.1) | copy-start | bytes 6291460
  0.6 73.6 %copy-start.2 = (s32[2048]{0:T(1024)S(1)}, s32[2048]{0:T(1024)}, u32[]{:S(2)}) copy-start(s32[2048]{0:T(1024)} %param.10) | copy-start | bytes 24580
  74.3 3.9 %copy-start.1 = (f32[512,512]{1,0:T(8,128)S(1)}, f32[512,512]{1,0:T(8,128)}, u32[]{:S(2)}) copy-start(f32[512,512]{1,0:T(8,128)} %get-tuple-element.8) | copy-start | bytes 3145732

commit v2 on v1

--- a/solution.py
+++ b/solution.py
@@ -10,7 +10,7 @@
 HEAD_DIM = 64
 PAD = 80
 PEERS = 4
-Y, NEAR, RELAYED, Z = range(PEERS)
+NEAR, Y, Z, RELAYED = range(PEERS)
 MESH = pl.DeviceIdType.MESH
 LOG2E = 1.4426950408889634
 NT = (((1,), (1,)), ((), ()))
@@ -19,7 +19,7 @@
 def window_kernel(
     n, mp, grid_ref, weight_ref, slot_ref, node_ref, peer_ref, gain_ref, w_ref, wo_ref,
     mesh_ref, returned_ref,
-    points, wcol, scaled, part, xg, gath, wbuf, wobuf, wvt, hot, rowm, colm,
+    points, wcol, scaled, part, xg, gath, wbuf, wobuf, wvt, hot, rowm,
     qm, kown, kbuf, vbuf, sbuf, acc, top, attb, out_part, in_part, total, state, back, ordered,
     local, gsem, wsem, asend, arecv, xsend, xrecv, psend, precv, msend, mrecv, rsend, rrecv,
     bsend, brecv,
@@ -38,11 +38,10 @@
     piece = count // peers
     odd = lax.rem(region, 2)
     far = lax.rem(region // 2, 2)
-    step = 2 - 4 * odd
     partner = region + 1 - 2 * odd
+    second = lax.rem(region + 2 - 4 * odd + n, n)
     across = region + 2 - 4 * far
     beyond = lax.rem(region + 4 - 8 * far + n, n)
-    second = lax.rem(region + step + n, n)
     relay_place = jnp.where(odd == far, Y, Z)
     cols = pl.ds(pl.multiple_of(core * width, width), width)
 
@@ -133,14 +132,115 @@
         NEAR: jnp.where(odd == 0, seen[2], seen[1]),
         RELAYED: jnp.where(odd == 0, seen[1], seen[2]),
     }
-    for ref, axis in ((rowm, 1), (colm, 0)):
-        shape = ref.shape[1:]
-        place = lax.broadcasted_iota(jnp.int32, shape, axis) // chunk
-        mask = jnp.zeros(shape, f32)
-        for p in range(peers):
-            mask = jnp.where(place == p, shown[p], mask)
-        ref[0] = jnp.ones(shape, f32)
-        ref[1] = mask
+    rowm[0] = jnp.ones(rowm.shape[1:], f32)
+    for p in range(peers):
+        rowm[1 + p] = jnp.full(rowm.shape[1:], shown[p], f32)
+    own.wait()
+
+    group = region * peers // n
+    turns = (
+        group,
+        group + 1 - 2 * lax.rem(group, 2),
+        jnp.where(group < 2, 2, 1),
+        jnp.where(group < 2, 3, 0),
+    )
+
+    def turn(c):
+        return turns[c]
+
+    def x_to_core(q, j):
+        span = pl.ds(pl.multiple_of(q * chunk, chunk), chunk)
+        return pltpu.make_async_remote_copy(
+            src_ref=xg.at[core, span],
+            dst_ref=xg.at[core, span],
+            send_sem=xsend.at[q, j],
+            recv_sem=xrecv.at[q, j],
+            device_id={"mp": lax.rem(core + j, mp)},
+            device_id_type=MESH,
+        )
+
+    def reap(c):
+        q = turn(c)
+
+        def one(k, carry):
+            source = q * (n // peers) + k
+
+            @pl.when(source != region)
+            def _():
+                pltpu.make_async_remote_copy(
+                    src_ref=part.at[0, pl.ds(0, cap)],
+                    dst_ref=xg.at[core, pl.ds(pl.multiple_of(source * cap, cap), cap)],
+                    send_sem=asend.at[0],
+                    recv_sem=arecv.at[source],
+                    device_id={"region": partner},
+                    device_id_type=MESH,
+                ).wait_recv()
+
+            return carry
+
+        lax.fori_loop(0, n // peers, one, 0)
+        for j in range(1, mp):
+            x_to_core(q, j).start()
+
+    def send(c, place, source, other):
+        return pltpu.make_async_remote_copy(
+            src_ref=source,
+            dst_ref=gath.at[1 + place, pl.ds(c * chunk, chunk), cols],
+            send_sem=psend.at[c, place],
+            recv_sem=precv.at[c, place],
+            device_id={"region": other},
+            device_id_type=MESH,
+        )
+
+    def own_chunk(c):
+        return gath.at[0, pl.ds(pl.multiple_of(turn(c) * chunk, chunk), chunk), cols]
+
+    def held(c, place):
+        return gath.at[1 + place, pl.ds(c * chunk, chunk), cols]
+
+    def to_near(c):
+        return send(c, NEAR, own_chunk(c), partner)
+
+    def to_across(c):
+        return send(c, Y, own_chunk(c), across)
+
+    def forward(c):
+        return send(c, Z, held(c, Y), beyond)
+
+    def relay(c):
+        if c >= peers - 1:
+            return send(c, RELAYED, held(c, NEAR), second)
+        return send(c, RELAYED, held(c, relay_place), partner)
+
+    def arrived(c, place):
+        pltpu.make_async_remote_copy(
+            src_ref=own_chunk(0),
+            dst_ref=held(c, place),
+            send_sem=psend.at[c, place],
+            recv_sem=precv.at[c, place],
+            device_id={"region": partner},
+            device_id_type=MESH,
+        ).wait_recv()
+
+    def normalise(c):
+        q = turn(c)
+        for j in range(1, mp):
+            x_to_core(q, j).wait_recv()
+        span = pl.ds(pl.multiple_of(q * chunk, chunk), chunk)
+        square = jnp.zeros((chunk, 1), f32)
+        for m in range(mp):
+            value = xg[m, span].astype(f32)
+            square += jnp.sum(value * value, axis=-1, keepdims=True)
+        inv = lax.rsqrt(square / (mp * width) + 1e-05)
+        for m in range(mp):
+            at = slice(m * width, (m + 1) * width)
+            gath[0, span, at] = (xg[m, span].astype(f32) * inv * gain_ref[:, at]).astype(bf16)
+        to_across(c).start()
+        to_near(c).start()
+
+    for c in range(2):
+        reap(c)
+        normalise(c)
     lane = lax.broadcasted_iota(jnp.int32, (n, rows), 1)
     spread = jnp.zeros((n, rows), jnp.int32)
     for c in range(cap):
@@ -153,100 +253,16 @@
     for load in weights:
         load.wait()
     wvt[...] = wbuf[2].T
-    own.wait()
-
-    def x_to_core(q, j):
-        span = pl.ds(pl.multiple_of(q * chunk, chunk), chunk)
-        return pltpu.make_async_remote_copy(
-            src_ref=xg.at[core, span],
-            dst_ref=xg.at[core, span],
-            send_sem=xsend.at[q, j],
-            recv_sem=xrecv.at[q, j],
-            device_id={"mp": lax.rem(core + j, mp)},
-            device_id_type=MESH,
-        )
-
-    def reaped(q, carry):
-        def one(k, c):
-            source = q * (n // peers) + k
-
-            @pl.when(source != region)
-            def _():
-                pltpu.make_async_remote_copy(
-                    src_ref=part.at[0, pl.ds(0, cap)],
-                    dst_ref=xg.at[core, pl.ds(pl.multiple_of(source * cap, cap), cap)],
-                    send_sem=asend.at[0],
-                    recv_sem=arecv.at[source],
-                    device_id={"region": partner},
-                    device_id_type=MESH,
-                ).wait_recv()
-
-            return c
-
-        lax.fori_loop(0, n // peers, one, 0)
-        for j in range(1, mp):
-            x_to_core(q, j).start()
-        return carry
-
-    lax.fori_loop(0, peers, reaped, 0)
-
-    def send(c, place, source, other):
-        return pltpu.make_async_remote_copy(
-            src_ref=source,
-            dst_ref=gath.at[1 + c, pl.ds(place * chunk, chunk), cols],
-            send_sem=psend.at[c, place],
-            recv_sem=precv.at[c, place],
-            device_id={"region": other},
-            device_id_type=MESH,
-        )
-
-    def own_chunk(c):
-        return gath.at[0, pl.ds(pl.multiple_of(c * chunk, chunk), chunk), cols]
-
-    def held(c, place):
-        return gath.at[1 + c, pl.ds(pl.multiple_of(place * chunk, chunk), chunk), cols]
-
-    def to_near(c):
-        return send(c, NEAR, own_chunk(c), partner)
-
-    def to_across(c):
-        return send(c, Y, own_chunk(c), across)
-
-    def forward(c):
-        return send(c, Z, held(c, Y), beyond)
-
-    def relay(c):
-        if c % 2 == 0:
-            return send(c, RELAYED, held(c, NEAR), second)
-        return send(c, RELAYED, held(c, relay_place), partner)
-
-    def arrived(c, place):
-        pltpu.make_async_remote_copy(
-            src_ref=own_chunk(0),
-            dst_ref=held(c, place),
-            send_sem=psend.at[c, place],
-            recv_sem=precv.at[c, place],
-            device_id={"region": partner},
-            device_id_type=MESH,
-        ).wait_recv()
-
-    def normalise(q, carry):
-        for j in range(1, mp):
-            x_to_core(q, j).wait_recv()
-        span = pl.ds(pl.multiple_of(q * chunk, chunk), chunk)
-        square = jnp.zeros((chunk, 1), f32)
-        for m in range(mp):
-            value = xg[m, span].astype(f32)
-            square += jnp.sum(value * value, axis=-1, keepdims=True)
-        inv = lax.rsqrt(square / (mp * width) + 1e-05)
-        for m in range(mp):
-            at = slice(m * width, (m + 1) * width)
-            gath[0, span, at] = (xg[m, span].astype(f32) * inv * gain_ref[:, at]).astype(bf16)
-        to_across(q).start()
-        to_near(q).start()
-        return carry
-
-    lax.fori_loop(0, peers, normalise, 0)
+    arrived(0, Y)
+    forward(0).start()
+    reap(2)
+    normalise(2)
+    arrived(1, Y)
+    forward(1).start()
+    reap(3)
+    normalise(3)
+    arrived(2, Y)
+    forward(2).start()
 
     def to_core(s, j):
         return pltpu.make_async_remote_copy(
@@ -268,8 +284,7 @@
             for j in range(1, mp):
                 to_core(s, j).wait_recv()
 
-        kind = jnp.minimum(s, 1)
-        seen = rowm[kind]
+        seen = rowm[s, :, :rows]
         keys = jnp.dot(gath[s], wbuf[1], preferred_element_type=f32)
 
         @pl.when(s == 0)
@@ -283,7 +298,7 @@
                 keep = (lane < HEAD_DIM) if h % 2 == 0 else (lane >= HEAD_DIM)
                 qm[h] = jnp.where(keep, pair, 0.0).astype(bf16)
 
-        kbuf[...] = jnp.where(colm[kind] > 0, keys, kown[...]).astype(bf16)
+        kbuf[...] = jnp.where(rowm[s, :, :width] > 0, keys, kown[...]).astype(bf16)
         turned = lax.dot_general(wvt[...], gath[s], NT, preferred_element_type=f32) * seen
         row = lax.broadcasted_iota(jnp.int32, (PAD - HEAD_DIM, rows), 0)
         extra = jnp.where(row == 0, jnp.broadcast_to(seen, row.shape), 0.0).astype(bf16)
@@ -318,40 +333,43 @@
                 summed = value if summed is None else summed + value
             acc[h] = acc[h] * jnp.exp2(old - new) + summed
             peak = after
-            if h == heads // 2 - 1:
-                for c in range(1, peers):
-
-                    @pl.when(s == c)
-                    def _(c=c):
-                        if c == 1:
-                            arrived(c, NEAR)
-                        if c == 3:
-                            arrived(c, NEAR)
-                        arrived_rest(c)
-                        complete(c + 1)
+            if h == max(heads // 2 - 1, 0):
+
+                @pl.when(s == 0)
+                def _():
+                    for c in range(3, peers):
+                        arrived(c, Y)
+                        forward(c).start()
+                    for c in range(peers):
+                        arrived(c, NEAR)
+                        if c >= peers - 1:
+                            relay(c).start()
+                    complete(1 + NEAR)
+                    complete(1 + Y)
+
+                @pl.when(s == 1)
+                def _():
+                    early(2)
+
+                @pl.when(s == 2)
+                def _():
+                    for c in range(peers):
+                        if c < peers - 1:
+                            late(c)
+                        else:
+                            arrived(c, Z)
+                    complete(1 + Z)
+
+                @pl.when(s == 3)
+                def _():
+                    for c in range(peers):
+                        arrived(c, RELAYED)
+                    complete(1 + RELAYED)
 
         @pl.when(s == 0)
         def _():
-            arrived(0, Y)
-            forward(0).start()
-            arrived(0, NEAR)
-            relay(0).start()
-            arrived(1, Y)
-            forward(1).start()
-            arrived(2, Y)
-            forward(2).start()
-            arrived(2, NEAR)
-            relay(2).start()
+            early(0)
             early(1)
-            arrived(0, Z)
-            arrived(0, RELAYED)
-            complete(1)
-            arrived(3, Y)
-            forward(3).start()
-
-        @pl.when(s == 1)
-        def _():
-            early(3)
 
         return carry
 
@@ -362,16 +380,10 @@
 
         relay(c).start()
 
-    def arrived_rest(c):
-        if c % 2 == 0:
+    def late(c):
+        @pl.when(relay_place != Z)
+        def _():
             arrived(c, Z)
-        else:
-
-            @pl.when(relay_place != Z)
-            def _():
-                arrived(c, Z)
-
-        arrived(c, RELAYED)
 
     lax.fori_loop(0, blocks, block, 0)
     for h in range(heads):
@@ -519,8 +531,7 @@
             pltpu.VMEM((width, depth), bf16),
             pltpu.VMEM((width, depth), bf16),
             pltpu.VMEM((rows, rows), bf16),
-            pltpu.VMEM((2, 1, rows), f32),
-            pltpu.VMEM((2, rows, 1), f32),
+            pltpu.VMEM((blocks, 1, max(rows, width)), f32),
             pltpu.VMEM((heads, rows, 2 * HEAD_DIM), bf16),
             pltpu.VMEM((rows, width), f32),
             pltpu.VMEM((rows, width), bf16),

time: 79.6 us -> 69.7 us (0.88)
  Pallas kernels: 73.6 us -> 64 us
    pallas_call x1, Pallas kernels: 73.6 us -> 64 us  [window(): pl.pallas_call(functools.partial(window_kernel, n, mp), out_shape=(jax.Sh...]
where the time goes in v2:
time: 69.7 us; the launch traced here: 69.6 us
  Pallas kernels  64 us (92%)
  matrix products  3.91 us (6%)
  local copies, waits for them, and re-layouts  0.98 us (1%)
    pallas_call x1, Pallas kernels, window(): pl.pallas_call(functools.partial(window_kernel, n, mp), out_shape=(jax.Sh...  64 us
    dot_general x1, matrix products, on_device(): gathered = jnp.dot(slot_hot.T, returned, preferred_element_type=jnp.float32)  3.91 us

profile of v2, /device:TPU:12, one launch (start us, length us, event | category | flops | bytes accessed | tf_op | source)
XLA Modules:
  0.0 69.6 jit_solution(15500852820096252201)
XLA Ops:
  0.6 0.0 copy-start
  0.6 0.0 copy-start.2
  0.7 64.0 %shard_map.95 = (f32[512,512]{1,0:T(8,128)}, bf16[512,512]{1,0:T(8,128)(2,1)}) custom-call(bf16[2048,512]{1,0:T(8,128)(2,1)} %grid_ref.1, f32[1,2048]{1,0:T(1,128)} %bitcast.4, s32[1,2048]{1,0:T(1,128)} %bitcast.5, s32[1,16,32]{2,1,0:T(8,128)} %node_ref.1, s32[1,4]{1,0:T(1,128)} %peer_ref.1, f32[1,1024]{1,0:T(1,128)} %bitcast.6, ...), custom_call_target="tpu_custom_call" | custom-call | tf_op jit(solution)/shard_map/pallas_call | solution.py:515
  64.6 0.0 copy-done
  64.7 0.0 copy-done.2
  64.7 0.0 copy-start.1
  64.7 3.9 %add_convert_fusion = bf16[2048,512]{1,0:T(8,128)(2,1)} fusion(bf16[2048,512]{1,0:T(8,128)(2,1)S(1)} %copy-done, bf16[512,512]{1,0:T(8,128)(2,1)} %get-tuple-element.5, s32[2048]{0:T(1024)S(1)} %copy-done.2), kind=kOutput, calls=%fused_computation | convolution fusion | flops 1077936128 | bytes 4726784 | tf_op jit(solution)/shard_map/dot_general | solution.py:580
  68.6 0.0 copy-done.1
  68.6 1.0 %copy.11 = f32[512,512]{1,0:T(8,128)} copy(f32[512,512]{1,0:T(8,128)S(1)} %copy-done.1) | data formatting | bytes 2097152
Async XLA Ops:
  0.6 64.0 %copy-start = (bf16[2048,512]{1,0:T(8,128)(2,1)S(1)}, bf16[2048,512]{1,0:T(8,128)(2,1)}, u32[]{:S(2)}) copy-start(bf16[2048,512]{1,0:T(8,128)(2,1)} %grid_ref.1) | copy-start | bytes 6291460
  0.6 64.0 %copy-start.2 = (s32[2048]{0:T(1024)S(1)}, s32[2048]{0:T(1024)}, u32[]{:S(2)}) copy-start(s32[2048]{0:T(1024)} %param.10) | copy-start | bytes 24580
  64.7 3.9 %copy-start.1 = (f32[512,512]{1,0:T(8,128)S(1)}, f32[512,512]{1,0:T(8,128)}, u32[]{:S(2)}) copy-start(f32[512,512]{1,0:T(8,128)} %get-tuple-element.8) | copy-start | bytes 3145732

commit v3 on v2

--- a/solution.py
+++ b/solution.py
@@ -427,11 +427,9 @@
         for j in range(1, mp):
             out_part[h, j] = product(h, lax.rem(core + j, mp))
             share(h, j).start()
-        span = span_of(h)
-        state[span] = xg[core, span].astype(f32) + product(h, core)
     for h in range(2):
         span = span_of(h)
-        value = state[span]
+        value = xg[core, span].astype(f32) + product(h, core)
         for j in range(1, mp):
             share(h, j).wait_recv()
             value += in_part[h, j]

time: 69.7 us -> 69.7 us (level)
  no operation moved by 1% of the time
where the time goes in v3:
time: 69.7 us; the launch traced here: 69.6 us
  Pallas kernels  64 us (92%)
  matrix products  3.92 us (6%)
  local copies, waits for them, and re-layouts  0.98 us (1%)
    pallas_call x1, Pallas kernels, window(): pl.pallas_call(functools.partial(window_kernel, n, mp), out_shape=(jax.Sh...  64 us
    dot_general x1, matrix products, on_device(): gathered = jnp.dot(slot_hot.T, returned, preferred_element_type=jnp.float32)  3.92 us

profile of v3, /device:TPU:12, one launch (start us, length us, event | category | flops | bytes accessed | tf_op | source)
XLA Modules:
  0.0 69.6 jit_solution(2233568773818755210)
XLA Ops:
  0.6 0.0 copy-start
  0.6 0.0 copy-start.2
  0.7 64.0 %shard_map.95 = (f32[512,512]{1,0:T(8,128)}, bf16[512,512]{1,0:T(8,128)(2,1)}) custom-call(bf16[2048,512]{1,0:T(8,128)(2,1)} %grid_ref.1, f32[1,2048]{1,0:T(1,128)} %bitcast.4, s32[1,2048]{1,0:T(1,128)} %bitcast.5, s32[1,16,32]{2,1,0:T(8,128)} %node_ref.1, s32[1,4]{1,0:T(1,128)} %peer_ref.1, f32[1,1024]{1,0:T(1,128)} %bitcast.6, ...), custom_call_target="tpu_custom_call" | custom-call | tf_op jit(solution)/shard_map/pallas_call | solution.py:513
  64.6 0.0 copy-done
  64.7 0.0 copy-done.2
  64.7 0.0 copy-start.1
  64.7 3.9 %add_convert_fusion = bf16[2048,512]{1,0:T(8,128)(2,1)} fusion(bf16[2048,512]{1,0:T(8,128)(2,1)S(1)} %copy-done, bf16[512,512]{1,0:T(8,128)(2,1)} %get-tuple-element.5, s32[2048]{0:T(1024)S(1)} %copy-done.2), kind=kOutput, calls=%fused_computation | convolution fusion | flops 1077936128 | bytes 4726784 | tf_op jit(solution)/shard_map/dot_general | solution.py:578
  68.6 0.0 copy-done.1
  68.6 1.0 %copy.11 = f32[512,512]{1,0:T(8,128)} copy(f32[512,512]{1,0:T(8,128)S(1)} %copy-done.1) | data formatting | bytes 2097152
Async XLA Ops:
  0.6 64.0 %copy-start = (bf16[2048,512]{1,0:T(8,128)(2,1)S(1)}, bf16[2048,512]{1,0:T(8,128)(2,1)}, u32[]{:S(2)}) copy-start(bf16[2048,512]{1,0:T(8,128)(2,1)} %grid_ref.1) | copy-start | bytes 6291460
  0.6 64.0 %copy-start.2 = (s32[2048]{0:T(1024)S(1)}, s32[2048]{0:T(1024)}, u32[]{:S(2)}) copy-start(s32[2048]{0:T(1024)} %param.10) | copy-start | bytes 24580
  64.7 3.9 %copy-start.1 = (f32[512,512]{1,0:T(8,128)S(1)}, f32[512,512]{1,0:T(8,128)}, u32[]{:S(2)}) copy-start(f32[512,512]{1,0:T(8,128)} %get-tuple-element.8) | copy-start | bytes 3145732
